TPU v7x, 32 devices: a whole 2x2x4 slice. The times are simulated.
32 devices in a mesh: section: 4 (over x, core), dp: 8 (over z, y).
Axes of the slice: x: 2, y: 2, z: 4, core: 2. Of those that a mesh axis runs over, the one named last changes fastest.
Arguments:
- activations: bfloat16 [1536, 8, 4096], P('dp', 'section'), may hold values from -8 to 8
- damping: float32 [8], P('section'), may hold values from 0.1 to 1
Outputs:
- schur_inverse: float32 [256, 128, 128], P(('section', 'dp'))
- coupling: float32 [256, 128, 128], P(('section', 'dp'))
All inputs are finite; a program needn't handle non-finite values.
Results may differ from a plain program's by a relative error of at most 0.0003.
Values may be sent and summed in bfloat16 or wider, within the bound.
A program may use at most 64 MiB of HBM per device.

v0:
```python
import jax
import jax.numpy as jnp
from jax import lax
from jax.sharding import PartitionSpec as P

B = 128


def passed_along(block, axis, distance):
    devices = range(lax.axis_size(axis))
    route = [(i - distance, i) for i in devices if i - distance in devices]
    return lax.ppermute(block, axis, route)


def solve_block(system, right_side):
    factor = jnp.linalg.cholesky(system)
    return jax.scipy.linalg.cho_solve((factor, True), right_side)


def local(activations, damping):
    token_rows, local_layers, model_width = activations.shape
    block_size = B
    blocks_layer = model_width // block_size
    group_size = lax.axis_size("dp")
    section_count = lax.axis_size("section")
    per_device = local_layers * blocks_layer // group_size
    tokens_all = token_rows * group_size
    flattened = activations.reshape(token_rows, local_layers * model_width)
    following_rows = passed_along(flattened[:, :model_width], "section", -1)
    next_layers = jnp.concatenate([flattened[:, model_width:], following_rows], axis=1)
    owner_layer = lax.axis_index("dp") * per_device // blocks_layer
    layer_index = jnp.arange(local_layers)
    sent_pairs = (
        flattened.reshape(token_rows, group_size, per_device * block_size),
        next_layers.reshape(token_rows, group_size, per_device * block_size),
    )
    left_cols, right_cols = (
        lax.all_to_all(sent_pairs[0], "dp", split_axis=1, concat_axis=0, tiled=True),
        lax.all_to_all(sent_pairs[1], "dp", split_axis=1, concat_axis=0, tiled=True),
    )
    left_cols = left_cols.reshape(tokens_all, per_device, block_size)
    right_cols = right_cols.reshape(tokens_all, per_device, block_size)
    diagonal_gram = (
        jnp.einsum("tgb,tgc->gbc", left_cols, left_cols, preferred_element_type=jnp.float32)
        / tokens_all
    )
    cross_gram = (
        jnp.einsum("tgb,tgc->gbc", left_cols, right_cols, preferred_element_type=jnp.float32)
        / tokens_all
    )
    owned_trace = jnp.sum(jnp.trace(diagonal_gram, axis1=1, axis2=2))
    traces = lax.psum(jnp.where(layer_index == owner_layer, owned_trace, 0.0), "dp")
    identity = jnp.eye(block_size, dtype=jnp.float32)
    damp_level = jnp.sum(jnp.where(layer_index == owner_layer, traces * damping, 0.0)) / model_width
    damped = diagonal_gram + damp_level * identity
    following_damped = passed_along(damped, ("section", "dp"), -(group_size // local_layers))
    final_layer = jnp.logical_and(
        lax.axis_index("section") == section_count - 1, owner_layer == local_layers - 1
    )
    system = jnp.where(final_layer, identity, following_damped)
    cross_gram = jnp.where(final_layer, jnp.zeros_like(cross_gram), cross_gram)
    coupling_t = jax.vmap(solve_block)(system, jnp.swapaxes(cross_gram, 1, 2))
    schur = damped - jnp.matmul(cross_gram, coupling_t, precision=lax.Precision.HIGHEST)
    identities = jnp.broadcast_to(identity, schur.shape)
    schur_inverse = jax.vmap(solve_block)(schur, identities)
    return (schur_inverse, jnp.swapaxes(coupling_t, 1, 2))


def solution(mesh):
    placed = (P("dp", "section", None), P("section"))
    return jax.shard_map(
        local,
        mesh=mesh,
        in_specs=placed,
        out_specs=(P(("section", "dp"), None, None), P(("section", "dp"), None, None)),
        check_vma=False,
    )
```

profile of v0, /device:TPU:0, one launch (start us, length us, event | category | flops | bytes accessed | tf_op | source)
XLA Modules:
  0.0 564.8 jit_solution(13872020890614534409)
XLA Ops:
  0.6 3.8 reshape_reshape.3
  4.4 3.4 copy.39
  7.8 7.6 %all-to-all-start = ((bf16[192,8,1024]{2,0,1:T(8,128)(2,1)}), bf16[192,8,1024]{2,0,1:T(8,128)(2,1)}, u32[]{:S(2)}, u32[]{:S(2)}) async-start(bf16[192,8,1024]{2,0,1:T(8,128)(2,1)} %copy.39), calls=%async_computation | async-start | bytes 6291456 | tf_op jit(solution)/shard_map/all_to_all | solution.py:38
  15.4 2.1 copy.64
  17.8 1.3 collective-permute-start
  19.1 4.0 collective-permute-done
  23.4 2.0 copy.85
  25.5 60.7 %all-to-all-done = bf16[192,8,1024]{2,0,1:T(8,128)(2,1)} async-done(((bf16[192,8,1024]{2,0,1:T(8,128)(2,1)}), bf16[192,8,1024]{2,0,1:T(8,128)(2,1)}, u32[]{:S(2)}, u32[]{:S(2)}) %all-to-all-start) | async-done | bytes 3145760 | tf_op jit(solution)/shard_map/all_to_all | solution.py:38
  86.2 3.6 all-to-all-start.1
  89.9 2.7 copy.63
  92.6 1.7 copy-done.1
  94.3 3.3 select_reduce_fusion.2
  98.3 58.9 %psum.7 = f32[2]{0:T(128)S(1)} all-reduce(f32[2]{0:T(128)S(1)} %compare_select_fusion.1), channel_id=1, replica_groups=mesh['section'=4,'dp'=8] {'dp'}, use_global_device_ids=true, to_apply=%region_1.2 | all-reduce | flops 2 | bytes 16 | tf_op jit(solution)/shard_map/psum | solution.py:52
  158.5 1.9 broadcast_add_fusion
  160.4 1.5 collective-permute-start.1
  161.9 34.5 %collective-permute-done.1 = f32[8,128,128]{1,2,0:T(8,128)} collective-permute-done((f32[8,128,128]{1,2,0:T(8,128)}, f32[8,128,128]{1,2,0:T(8,128)}, u32[]{:S(2)}, u32[]{:S(2)}) %collective-permute-start.1) | collective-permute-done | bytes 524320 | tf_op jit(solution)/shard_map/ppermute | solution.py:12
  196.4 1.9 broadcast_select_fusion
  198.3 2.1 copy.47
  200.3 2.1 fusion.27
  202.4 95.2 %custom-call.10 = f32[8,128,128]{2,1,0:T(8,128)} custom-call(f32[8,128,128]{2,1,0:T(8,128)} %fusion.27), custom_call_target="Cholesky" | custom-call | tf_op jit(solution)/shard_map/vmap(jit(cholesky))/cholesky | solution.py:16
  297.6 1.1 select_reduce_fusion.1
  298.8 2.0 select_bitcast_fusion.1
  300.8 80.0 %custom-call.11 = f32[8,1,128,128]{2,3,1,0:T(8,128)} custom-call(f32[8,1,128,128]{3,2,1,0:T(8,128)} %select_bitcast_fusion.1), custom_call_target="InvertDiagBlocksLowerTriangular" | custom-call | tf_op jit(solution)/shard_map/vmap(jit(_cho_solve))/triangular_solve | solution.py:17
  381.7 1.0 copy-done.2
  382.7 1.9 fusion.13
  384.6 1.0 fusion.25
  386.3 2.0 convolution_subtract_fusion
  388.4 1.0 copy.54
  389.6 93.8 %custom-call.12 = f32[8,128,128]{2,1,0:T(8,128)S(1)} custom-call(f32[8,128,128]{2,1,0:T(8,128)S(1)} %fusion.22), custom_call_target="Cholesky" | custom-call | tf_op jit(solution)/shard_map/vmap(jit(cholesky))/cholesky | solution.py:16
  483.7 78.6 %custom-call.13 = f32[8,1,128,128]{2,3,1,0:T(8,128)S(1)} custom-call(f32[8,1,128,128]{3,2,1,0:T(8,128)S(1)} %select_bitcast_fusion), custom_call_target="InvertDiagBlocksLowerTriangular" | custom-call | tf_op jit(solution)/shard_map/vmap(jit(_cho_solve))/triangular_solve | solution.py:17
  562.3 1.0 fusion.20
  563.3 1.4 fusion.18
  (26 shorter events, 4.1 us)
Async XLA Ops:
  7.8 7.6 %copy-start = (bf16[192,2,4096]{2,1,0:T(2,128)(2,1)S(1)}, bf16[192,2,4096]{2,1,0:T(2,128)(2,1)}, u32[]{:S(2)}) copy-start(bf16[192,2,4096]{2,1,0:T(2,128)(2,1)} %param.5) | copy-start | bytes 9437188
  7.8 78.4 %all-to-all-start = ((bf16[192,8,1024]{2,0,1:T(8,128)(2,1)}), bf16[192,8,1024]{2,0,1:T(8,128)(2,1)}, u32[]{:S(2)}, u32[]{:S(2)}) async-start(bf16[192,8,1024]{2,0,1:T(8,128)(2,1)} %copy.39), calls=%async_computation | async-start | bytes 6291456 | tf_op jit(solution)/shard_map/all_to_all | solution.py:38
  17.8 5.3 collective-permute-start
  86.2 294.6 %all-to-all-start.1 = ((bf16[192,8,1024]{2,0,1:T(8,128)(2,1)}), bf16[192,8,1024]{2,0,1:T(8,128)(2,1)S(1)}, u32[]{:S(2)}, u32[]{:S(2)}) async-start(bf16[192,8,1024]{2,0,1:T(8,128)(2,1)} %bitcast.49), calls=%async_computation.1 | async-start | bytes 6291456 | tf_op jit(solution)/shard_map/all_to_all | solution.py:39
  92.6 1.7 copy-start.1
  92.6 64.6 %copy-start.4 = (f32[2]{0:T(128)S(1)}, f32[2]{0:T(128)}, u32[]{:S(2)}) copy-start(f32[2]{0:T(128)} %param.6) | copy-start | bytes 28
  160.4 36.0 %collective-permute-start.1 = (f32[8,128,128]{1,2,0:T(8,128)}, f32[8,128,128]{1,2,0:T(8,128)}, u32[]{:S(2)}, u32[]{:S(2)}) collective-permute-start(f32[8,128,128]{1,2,0:T(8,128)} %broadcast_add_fusion), channel_id=1, source_target_pairs={{4,0},{5,1},{6,2},{7,3},{8,4},{9,5},{10,6},{11,7},{12,8},{13,9},{1... | collective-permute-start | bytes 1572872 | tf_op jit(solution)/shard_map/ppermute | solution.py:12
  380.8 1.9 copy-start.2
  382.7 1.9 copy-start.3
where the time goes:
time: 566 us; the launch traced here: 565 us
  other arithmetic  359 us (63%)
  waiting for transfers between devices  99.2 us (18%)
  blocking collectives  58.9 us (10%)
  local copies, waits for them, and re-layouts  21.2 us (4%)
  starting transfers between devices  14 us (2%)
  matrix products  11.3 us (2%)
    another operation x7, other arithmetic, solve_block(): factor = jnp.linalg.cholesky(system)  190 us
    another operation x5, other arithmetic, solve_block(): return jax.scipy.linalg.cho_solve((factor, True), right_side)  161 us
    all_to_all x1, waiting for transfers between devices, local(): lax.all_to_all(sent_pairs[0], 'dp', split_axis=1, concat_axis=0, tiled=True)  60.7 us
    psum x1, blocking collectives, local(): lax.psum(jnp.where(layer_index == owner_layer, owned_trace, 0.0), 'dp')  58.9 us
    ppermute x2, waiting for transfers between devices, passed_along(): return lax.ppermute(block, axis, route)  38.5 us
  transfers between devices with their start and end apart: 4, of which 3 were waited for; matrix products, arithmetic and copies ran while one was open for 35% of the time, Pallas kernels for 0%

commit v1 on v0

v1 whole, which is shorter than its diff:
```python
import functools

import jax
import jax.numpy as jnp
from jax import lax
from jax.experimental import pallas as pl
from jax.experimental.pallas import tpu as pltpu
from jax.sharding import PartitionSpec as P

B = 128
PANEL = 8


def passed_along(block, axis, distance):
    devices = range(lax.axis_size(axis))
    route = [(i - distance, i) for i in devices if i - distance in devices]
    return lax.ppermute(block, axis, route)


def invert_in_place(work, count, size):
    lane = lax.broadcasted_iota(jnp.int32, (count, size), 1)

    def step(_, carry):
        rows = [work[k * count : (k + 1) * count, :] for k in range(PANEL)]
        for k in range(PANEL):
            pivot = jnp.where(lane == k, 1.0, rows[k]) * (1.0 / rows[k][:, k : k + 1])
            for i in range(PANEL):
                if i != k:
                    rows[i] = jnp.where(lane == k, 0.0, rows[i]) - rows[i][:, k : k + 1] * pivot
            rows[k] = pivot
        for i in range(PANEL, size):
            row = work[i * count : (i + 1) * count, :]
            total = jnp.where(lane < PANEL, 0.0, row)
            for k in range(PANEL):
                total = total - row[:, k : k + 1] * rows[k]
            to = (i - PANEL) * count
            work[to : to + count, :] = pltpu.roll(total, size - PANEL, 1)
        for k in range(PANEL):
            to = (size - PANEL + k) * count
            work[to : to + count, :] = pltpu.roll(rows[k], size - PANEL, 1)
        return carry

    lax.fori_loop(0, size // PANEL, step, 0)


def blocks_kernel(count, tokens, levels, left, right, inverse, coupling, work, damped, cross):
    size = B
    identity = (
        lax.broadcasted_iota(jnp.int32, (size, size), 0)
        == lax.broadcasted_iota(jnp.int32, (size, size), 1)
    ).astype(jnp.float32)
    own_level, next_level, final = levels[0], levels[1], levels[2]
    exact = dict(preferred_element_type=jnp.float32, precision=lax.Precision.HIGHEST)

    for b in range(count):
        cols = slice(b * size, (b + 1) * size)
        both = jnp.concatenate([left[:, cols], right[:, cols]], axis=1)
        gram = lax.dot_general(
            both, both, (((0,), (0,)), ((), ())), preferred_element_type=jnp.float32
        ) / tokens
        damped[b] = gram[:size, :size] + own_level * identity
        cross[b] = jnp.where(final > 0.5, 0.0, gram[:size, size:])
        following = gram[size:, size:] + next_level * identity
        work[pl.ds(b, size, stride=count), :] = jnp.where(final > 0.5, identity, following)
    invert_in_place(work, count, size)
    for b in range(count):
        following_inverse = work[pl.ds(b, size, stride=count), :]
        coupled = jnp.dot(cross[b], following_inverse, **exact)
        coupling[b] = coupled
        taken = lax.dot_general(coupled, cross[b], (((1,), (1,)), ((), ())), **exact)
        work[pl.ds(b, size, stride=count), :] = damped[b] - taken
    invert_in_place(work, count, size)
    for b in range(count):
        inverse[b] = work[pl.ds(b, size, stride=count), :]


def local(activations, damping):
    token_rows, local_layers, model_width = activations.shape
    block_size = B
    blocks_layer = model_width // block_size
    group_size = lax.axis_size("dp")
    section_count = lax.axis_size("section")
    per_device = local_layers * blocks_layer // group_size
    tokens_all = token_rows * group_size
    owner_layer = lax.axis_index("dp") * per_device // blocks_layer

    squares = jnp.sum(jnp.square(activations.astype(jnp.float32)), axis=(0, 2))
    levels = damping * lax.psum(squares, "dp") / (tokens_all * model_width)
    levels = jnp.concatenate([levels, passed_along(levels[:1], "section", -1)])
    final_layer = jnp.logical_and(
        lax.axis_index("section") == section_count - 1, owner_layer == local_layers - 1
    )
    scalars = jnp.stack(
        [
            lax.dynamic_index_in_dim(levels, owner_layer, 0, keepdims=False),
            lax.dynamic_index_in_dim(levels, owner_layer + 1, 0, keepdims=False),
            final_layer.astype(jnp.float32),
        ]
    )

    flattened = activations.reshape(token_rows, local_layers * model_width)
    following_rows = passed_along(flattened[:, :model_width], "section", -1)
    next_layers = jnp.concatenate([flattened[:, model_width:], following_rows], axis=1)
    sent_pairs = (
        flattened.reshape(token_rows, group_size, per_device * block_size),
        next_layers.reshape(token_rows, group_size, per_device * block_size),
    )
    left_cols, right_cols = (
        lax.all_to_all(sent_pairs[0], "dp", split_axis=1, concat_axis=0, tiled=True),
        lax.all_to_all(sent_pairs[1], "dp", split_axis=1, concat_axis=0, tiled=True),
    )
    left_cols = left_cols.reshape(tokens_all, per_device * block_size)
    right_cols = right_cols.reshape(tokens_all, per_device * block_size)

    out = jax.ShapeDtypeStruct((per_device, block_size, block_size), jnp.float32)
    vmem = pl.BlockSpec(memory_space=pltpu.VMEM)
    return pl.pallas_call(
        functools.partial(blocks_kernel, per_device, tokens_all),
        out_shape=(out, out),
        in_specs=[pl.BlockSpec(memory_space=pltpu.SMEM), vmem, vmem],
        out_specs=(vmem, vmem),
        scratch_shapes=[
            pltpu.VMEM((block_size * per_device, block_size), jnp.float32),
            pltpu.VMEM((per_device, block_size, block_size), jnp.float32),
            pltpu.VMEM((per_device, block_size, block_size), jnp.float32),
        ],
        compiler_params=pltpu.CompilerParams(vmem_limit_bytes=48 * 1024 * 1024),
    )(scalars, left_cols, right_cols)


def solution(mesh):
    placed = (P("dp", "section", None), P("section"))
    return jax.shard_map(
        local,
        mesh=mesh,
        in_specs=placed,
        out_specs=(P(("section", "dp"), None, None), P(("section", "dp"), None, None)),
        check_vma=False,
    )
```

time: 566 us -> 412 us (0.73)
  the two profiles are of different devices: /device:TPU:0 before, /device:TPU:9 now
where the time goes in v1:
time: 412 us; the launch traced here: 411 us
  Pallas kernels  237 us (58%)
  blocking collectives  66.5 us (16%)
  waiting for transfers between devices  61.3 us (15%)
  starting transfers between devices  21.4 us (5%)
  local copies, waits for them, and re-layouts  14 us (3%)
  other arithmetic  10.7 us (3%)
    pallas_call x1, Pallas kernels, local(): pl.pallas_call(functools.partial(blocks_kernel, per_device, tokens_all),...  237 us
    psum x1, blocking collectives, local(): levels = damping * lax.psum(squares, 'dp') / (tokens_all * model_width)  66.5 us
    all_to_all x1, waiting for transfers between devices, local(): lax.all_to_all(sent_pairs[0], 'dp', split_axis=1, concat_axis=0, tiled=True)  39.8 us
    ppermute x2, waiting for transfers between devices, passed_along(): return lax.ppermute(block, axis, route)  21.5 us
    ppermute x2, starting transfers between devices, passed_along(): return lax.ppermute(block, axis, route)  10.2 us
    reduce_sum x1, other arithmetic, local(): squares = jnp.sum(jnp.square(activations.astype(jnp.float32)), axis=(0, 2))  8.48 us
  transfers between devices with their start and end apart: 4, of which 3 were waited for; matrix products, arithmetic and copies ran while one was open for 4% of the time, Pallas kernels for 0%

profile of v1, /device:TPU:9, one launch (start us, length us, event | category | flops | bytes accessed | tf_op | source)
XLA Modules:
  0.0 411.3 jit_solution(17791986277688434453)
XLA Ops:
  0.6 3.8 reshape_reshape.3
  4.4 3.4 copy.7
  7.8 5.7 %all-to-all-start = ((bf16[192,8,1024]{2,0,1:T(8,128)(2,1)}), bf16[192,8,1024]{2,0,1:T(8,128)(2,1)S(1)}, u32[]{:S(2)}, u32[]{:S(2)}) async-start(bf16[192,8,1024]{2,0,1:T(8,128)(2,1)} %copy.7), calls=%async_computation | async-start | bytes 6291456 | tf_op jit(solution)/shard_map/all_to_all | solution.py:109
  13.5 4.0 copy.10
  17.5 0.3 fusion
  17.7 3.1 collective-permute-start.1
  20.9 19.5 %collective-permute-done.1 = bf16[192,4096]{1,0:T(8,128)(2,1)S(1)} collective-permute-done((bf16[192,4096]{1,0:T(8,128)(2,1)S(1)}, bf16[192,4096]{1,0:T(8,128)(2,1)S(1)}, u32[]{:S(2)}, u32[]{:S(2)}) %collective-permute-start.1) | collective-permute-done | bytes 1572896 | tf_op jit(solution)/shard_map/ppermute | solution.py:17
  40.4 0.3 pad_maximum_fusion
  40.7 2.0 copy.12
  42.7 39.8 %all-to-all-done = bf16[192,8,1024]{2,0,1:T(8,128)(2,1)S(1)} async-done(((bf16[192,8,1024]{2,0,1:T(8,128)(2,1)}), bf16[192,8,1024]{2,0,1:T(8,128)(2,1)S(1)}, u32[]{:S(2)}, u32[]{:S(2)}) %all-to-all-start) | async-done | bytes 3145760 | tf_op jit(solution)/shard_map/all_to_all | solution.py:109
  82.5 5.5 %all-to-all-start.1 = ((bf16[192,8,1024]{2,0,1:T(8,128)(2,1)}), bf16[192,8,1024]{2,0,1:T(8,128)(2,1)}, u32[]{:S(2)}, u32[]{:S(2)}) async-start(bf16[192,8,1024]{2,0,1:T(8,128)(2,1)} %bitcast.20), calls=%async_computation.1 | async-start | bytes 6291456 | tf_op jit(solution)/shard_map/all_to_all | solution.py:110
  88.0 0.0 copy-start
  88.0 8.5 %multiply_reduce_fusion = f32[2]{0:T(128)S(1)} fusion(bf16[192,2,4096]{2,1,0:T(2,128)(2,1)} %param.2), kind=kLoop, calls=%fused_computation | loop fusion | flops 4718590 | bytes 3145736 | tf_op jit(solution)/shard_map/reduce_sum | solution.py:87
  96.5 66.5 %psum.7 = f32[2]{0:T(128)S(1)} all-reduce(f32[2]{0:T(128)S(1)} %multiply_reduce_fusion), channel_id=1, replica_groups=mesh['section'=4,'dp'=8] {'dp'}, use_global_device_ids=true, to_apply=%region_1.2 | all-reduce | flops 2 | bytes 16 | tf_op jit(solution)/shard_map/psum | solution.py:88
  163.0 0.0 copy-done
  163.0 7.0 %collective-permute-start = (f32[1]{0:T(128)S(1)}, f32[1]{0:T(128)}, u32[]{:S(2)}, u32[]{:S(2)}) collective-permute-start(f32[1]{0:T(128)S(1)} %bitcast.23), channel_id=1, source_target_pairs={{8,0},{16,8},{24,16},{9,1},{17,9},{25,17},{10,2},{18,10},{26,18},{... | collective-permute-start | bytes 20 | tf_op jit(solution)/shard_map/ppermute | solution.py:17
  170.1 2.0 collective-permute-done
  172.1 0.6 pad_maximum_fusion.1
  172.8 0.6 fusion.1
  173.3 1.3 pad_maximum_fusion.2.levels
  174.6 0.0 all-to-all-done.1
  174.6 236.6 %shard_map.41 = (f32[8,128,128]{2,1,0:T(8,128)}, f32[8,128,128]{2,1,0:T(8,128)}) custom-call(f32[3]{0:T(128)S(1)} %pad_maximum_fusion.2.levels, bf16[1536,1024]{1,0:T(8,128)(2,1)S(1)} %bitcast.18, bf16[1536,1024]{1,0:T(8,128)(2,1)} %bitcast.6.right), custom_call_target="tpu_custom_call" | custom-call | tf_op jit(solution)/shard_map/pallas_call | solution.py:117
  (1 shorter events, 0.0 us)
Async XLA Ops:
  7.8 74.7 %all-to-all-start = ((bf16[192,8,1024]{2,0,1:T(8,128)(2,1)}), bf16[192,8,1024]{2,0,1:T(8,128)(2,1)S(1)}, u32[]{:S(2)}, u32[]{:S(2)}) async-start(bf16[192,8,1024]{2,0,1:T(8,128)(2,1)} %copy.7), calls=%async_computation | async-start | bytes 6291456 | tf_op jit(solution)/shard_map/all_to_all | solution.py:109
  17.7 22.6 %collective-permute-start.1 = (bf16[192,4096]{1,0:T(8,128)(2,1)S(1)}, bf16[192,4096]{1,0:T(8,128)(2,1)S(1)}, u32[]{:S(2)}, u32[]{:S(2)}) collective-permute-start(bf16[192,4096]{1,0:T(8,128)(2,1)S(1)} %get-tuple-element.3), channel_id=1, source_target_pairs={{8,0},{16,8},{24,16},{9,1},{17,9},{25,17},{10,2},{18,10},{26,18},{... | collective-permute-start | bytes 4718600 | tf_op jit(solution)/shard_map/ppermute | solution.py:17
  82.5 92.1 %all-to-all-start.1 = ((bf16[192,8,1024]{2,0,1:T(8,128)(2,1)}), bf16[192,8,1024]{2,0,1:T(8,128)(2,1)}, u32[]{:S(2)}, u32[]{:S(2)}) async-start(bf16[192,8,1024]{2,0,1:T(8,128)(2,1)} %bitcast.20), calls=%async_computation.1 | async-start | bytes 6291456 | tf_op jit(solution)/shard_map/all_to_all | solution.py:110
  88.0 75.0 %copy-start = (f32[2]{0:T(128)S(1)}, f32[2]{0:T(128)}, u32[]{:S(2)}) copy-start(f32[2]{0:T(128)} %param.3) | copy-start | bytes 28
  163.0 9.1 %collective-permute-start = (f32[1]{0:T(128)S(1)}, f32[1]{0:T(128)}, u32[]{:S(2)}, u32[]{:S(2)}) collective-permute-start(f32[1]{0:T(128)S(1)} %bitcast.23), channel_id=1, source_target_pairs={{8,0},{16,8},{24,16},{9,1},{17,9},{25,17},{10,2},{18,10},{26,18},{... | collective-permute-start | bytes 20 | tf_op jit(solution)/shard_map/ppermute | solution.py:17

commit v2 on v1

v2 whole, which is shorter than its diff:
```python
import functools

import jax
import jax.numpy as jnp
from jax import lax
from jax.experimental import pallas as pl
from jax.experimental.pallas import tpu as pltpu
from jax.sharding import PartitionSpec as P

B = 128
PANEL = 8


def passed_along(block, axis, distance):
    devices = range(lax.axis_size(axis))
    route = [(i - distance, i) for i in devices if i - distance in devices]
    return lax.ppermute(block, axis, route)


def three_terms(value):
    high = value.astype(jnp.bfloat16).astype(jnp.float32)
    rest = value - high
    middle = rest.astype(jnp.bfloat16).astype(jnp.float32)
    return high, middle, rest - middle


def invert_in_place(work, panel, count, size):
    lane = lax.broadcasted_iota(jnp.int32, (count, size), 1)
    panel_lane = lax.broadcasted_iota(jnp.int32, (PANEL, size), 1)
    panel_row = lax.broadcasted_iota(jnp.int32, (PANEL, size), 0)
    full_lane = lax.broadcasted_iota(jnp.int32, (size, size), 1)
    full_row = lax.broadcasted_iota(jnp.int32, (size, size), 0)

    def step(s, carry):
        first = pl.multiple_of(s * PANEL, PANEL)
        rows, entries = [], []
        for k in range(PANEL):
            row = pltpu.roll(work[pl.ds(first + k, count, stride=size), :], size - first, 1)
            entries.append(
                [jnp.broadcast_to(row[:, j : j + 1], row.shape) for j in range(PANEL)]
            )
            rows.append(jnp.where(lane == k, 1.0, jnp.where(lane < PANEL, 0.0, row)))
        for k in range(PANEL):
            scale = 1.0 / entries[k][k]
            rows[k] = rows[k] * scale
            for j in range(k + 1, PANEL):
                entries[k][j] = entries[k][j] * scale
            for i in range(PANEL):
                if i != k:
                    factor = entries[i][k]
                    rows[i] = rows[i] - factor * rows[k]
                    for j in range(k + 1, PANEL):
                        entries[i][j] = entries[i][j] - factor * entries[k][j]
        for k in range(PANEL):
            panel[pl.ds(k, count, stride=PANEL), :] = pltpu.roll(rows[k], first, 1)
        local_lane = panel_lane - first
        in_panel = jnp.logical_and(local_lane >= 0, local_lane < PANEL)
        own = jnp.where(local_lane == panel_row, -1.0, 0.0)
        replaced = jnp.logical_or(
            jnp.logical_and(full_lane >= first, full_lane < first + PANEL),
            jnp.logical_and(full_row >= first, full_row < first + PANEL),
        )
        for b in range(count):
            old = work[pl.ds(b * size + first, PANEL), :]
            column = jnp.where(in_panel, own, jnp.where(local_lane < 0, -old, old))
            ch, cm, cl = three_terms(column)
            rh, rm, rl = three_terms(panel[b * PANEL : (b + 1) * PANEL, :])
            left = jnp.concatenate([ch, ch, ch, cm, cm, cl], axis=0).astype(jnp.bfloat16)
            right = jnp.concatenate([rh, rm, rl, rh, rm, rh], axis=0).astype(jnp.bfloat16)
            update = lax.dot_general(
                left, right, (((0,), (0,)), ((), ())), preferred_element_type=jnp.float32
            )
            at = slice(b * size, (b + 1) * size)
            work[at, :] = jnp.where(replaced, 0.0, work[at, :]) - update
        return carry

    lax.fori_loop(0, size // PANEL, step, 0)


def coupling_kernel(count, spread, tokens, levels, left, right, schur, coupling, work, panel, cross):
    size = B
    layers = count // spread
    identity = (
        lax.broadcasted_iota(jnp.int32, (size, size), 0)
        == lax.broadcasted_iota(jnp.int32, (size, size), 1)
    ).astype(jnp.float32)
    exact = dict(preferred_element_type=jnp.float32, precision=lax.Precision.HIGHEST)

    def cols(b):
        source, at = (left, b) if b < count else (right, b - count)
        return source[:, at * size : (at + 1) * size]

    for b in range(count):
        layer = b // spread
        both = jnp.concatenate([cols(b), cols(b + spread)], axis=1)
        gram = lax.dot_general(
            both, both, (((0,), (0,)), ((), ())), preferred_element_type=jnp.float32
        ) / tokens
        crossed = gram[:size, size:]
        following = gram[size:, size:] + levels[layer + 1] * identity
        if layer == layers - 1:
            final = levels[layers + 1] > 0.5
            crossed = jnp.where(final, 0.0, crossed)
            following = jnp.where(final, identity, following)
        schur[b] = gram[:size, :size] + levels[layer] * identity
        cross[b] = crossed
        work[b * size : (b + 1) * size, :] = following
    invert_in_place(work, panel, count, size)
    for b in range(count):
        coupled = jnp.dot(cross[b], work[b * size : (b + 1) * size, :], **exact)
        coupling[b] = coupled
        taken = lax.dot_general(coupled, cross[b], (((1,), (1,)), ((), ())), **exact)
        schur[b] = schur[b] - taken


def inverse_kernel(count, schur, inverse, panel):
    inverse[...] = schur[...]
    invert_in_place(inverse, panel, count, B)


def local(activations, damping):
    token_rows, local_layers, model_width = activations.shape
    block_size = B
    blocks_layer = model_width // block_size
    group_size = lax.axis_size("dp")
    section_count = lax.axis_size("section")
    per_device = local_layers * blocks_layer // group_size
    tokens_all = token_rows * group_size
    last_section = (lax.axis_index("section") == section_count - 1).astype(jnp.float32)

    squares = jnp.sum(jnp.square(activations.astype(jnp.float32)), axis=(0, 2))
    levels = damping * lax.psum(squares, "dp") / (tokens_all * model_width)
    levels = jnp.concatenate([levels, passed_along(levels[:1], "section", -1)])

    every_layer = per_device % local_layers == 0 and group_size % local_layers == 0
    if every_layer:
        spread = per_device // local_layers
        groups = group_size // local_layers
        sent = activations.reshape(
            token_rows, local_layers, groups, local_layers, spread * block_size
        )
        sent = sent.transpose(0, 3, 2, 1, 4).reshape(token_rows, group_size, -1)
        left_cols = lax.all_to_all(sent, "dp", split_axis=1, concat_axis=0, tiled=True)
        left_cols = left_cols.reshape(tokens_all, per_device * block_size)
        right_cols = passed_along(left_cols[:, : spread * block_size], "section", -1)
        scalars = jnp.concatenate([levels, last_section[None]])
    else:
        spread = per_device
        owner_layer = lax.axis_index("dp") * per_device // blocks_layer
        flattened = activations.reshape(token_rows, local_layers * model_width)
        following_rows = passed_along(flattened[:, :model_width], "section", -1)
        next_layers = jnp.concatenate([flattened[:, model_width:], following_rows], axis=1)
        left_cols, right_cols = (
            lax.all_to_all(
                sent.reshape(token_rows, group_size, -1), "dp", split_axis=1, concat_axis=0, tiled=True
            ).reshape(tokens_all, per_device * block_size)
            for sent in (flattened, next_layers)
        )
        last_layer = (owner_layer == local_layers - 1).astype(jnp.float32)
        scalars = jnp.concatenate(
            [lax.dynamic_slice(levels, (owner_layer,), (2,)), (last_section * last_layer)[None]]
        )

    blocks = (per_device, block_size, block_size)
    out = jax.ShapeDtypeStruct(blocks, jnp.float32)
    flat = jax.ShapeDtypeStruct((per_device * block_size, block_size), jnp.float32)
    vmem = pl.BlockSpec(memory_space=pltpu.VMEM)
    panel = pltpu.VMEM((per_device * PANEL, block_size), jnp.float32)
    schur, coupling = pl.pallas_call(
        functools.partial(coupling_kernel, per_device, spread, tokens_all),
        out_shape=(out, out),
        in_specs=[pl.BlockSpec(memory_space=pltpu.SMEM), vmem, vmem],
        out_specs=(vmem, vmem),
        scratch_shapes=[
            pltpu.VMEM(flat.shape, jnp.float32),
            panel,
            pltpu.VMEM(blocks, jnp.float32),
        ],
        compiler_params=pltpu.CompilerParams(vmem_limit_bytes=48 * 1024 * 1024),
    )(scalars, left_cols, right_cols)
    inverse = pl.pallas_call(
        functools.partial(inverse_kernel, per_device),
        out_shape=flat,
        in_specs=[vmem],
        out_specs=vmem,
        scratch_shapes=[panel],
        cost_estimate=pl.CostEstimate(
            flops=12 * per_device * block_size**3, bytes_accessed=40_000_000, transcendentals=0
        ),
    )(schur.reshape(flat.shape)).reshape(blocks)

    if every_layer:
        owners = [[h * groups + g for h in range(local_layers)] for g in range(groups)]
        inverse, coupling = (
            lax.all_to_all(
                x, "dp", split_axis=0, concat_axis=0, tiled=True, axis_index_groups=owners
            )
            for x in (inverse, coupling)
        )
    return inverse, coupling


def solution(mesh):
    placed = (P("dp", "section", None), P("section"))
    return jax.shard_map(
        local,
        mesh=mesh,
        in_specs=placed,
        out_specs=(P(("section", "dp"), None, None), P(("section", "dp"), None, None)),
        check_vma=False,
    )
```

time: 412 us -> 228 us (0.55)
  the two profiles are of different devices: /device:TPU:9 before, /device:TPU:0 now
where the time goes in v2:
time: 228 us; the launch traced here: 227 us
  blocking collectives  130 us (57%)
  Pallas kernels  65.4 us (29%)
  local copies, waits for them, and re-layouts  18.8 us (8%)
  other arithmetic  7.35 us (3%)
  starting transfers between devices  2.88 us (1%)
    all_to_all x1, blocking collectives, local(): lax.all_to_all(sent, 'dp', split_axis=1, concat_axis=0, tiled=True)  78 us
    pallas_call x1, Pallas kernels, local(): pl.pallas_call(functools.partial(coupling_kernel, per_device, spread, tok...  34.4 us
    all_to_all x2, blocking collectives, local(): lax.all_to_all(x, 'dp', split_axis=0, concat_axis=0, tiled=True, axis_ind...  33 us
    pallas_call x1, Pallas kernels, local(): pl.pallas_call(functools.partial(inverse_kernel, per_device), out_shape=f...  31 us
    psum x1, blocking collectives, local(): levels = damping * lax.psum(squares, 'dp') / (tokens_all * model_width)  19.4 us
    reduce_sum x1, other arithmetic, local(): squares = jnp.sum(jnp.square(activations.astype(jnp.float32)), axis=(0, 2))  6.58 us
    reshape x1, local copies, waits for them, and re-layouts, local(): activations.reshape(token_rows, local_layers, groups, local_layers, sprea...  6.16 us
  transfers between devices with their start and end apart: 2, of which 1 were waited for; matrix products, arithmetic and copies ran while one was open for 3% of the time, Pallas kernels for 0%

profile of v2, /device:TPU:0, one launch (start us, length us, event | category | flops | bytes accessed | tf_op | source)
XLA Modules:
  0.0 227.2 jit_solution(11649222112127641397)
XLA Ops:
  0.6 6.2 %reshape.20 = bf16[192,2,4,2,512]{4,3,2,1,0:T(2,128)(2,1)} reshape(bf16[192,2,4096]{2,1,0:T(2,128)(2,1)} %param.2) | data formatting | bytes 6291456 | tf_op jit(solution)/shard_map/reshape | solution.py:139
  6.8 4.3 %copy.4 = bf16[192,2,4,2,512]{4,3,0,2,1:T(2,128)(2,1)S(1)} copy(bf16[192,2,4,2,512]{4,1,2,3,0:T(2,128)(2,1)} %bitcast.15) | data formatting | bytes 6291456 | tf_op jit(solution)/shard_map/transpose | solution.py:142
  11.1 3.9 %reshape.21 = bf16[192,8,1024]{2,0,1:T(8,128)(2,1)} reshape(bf16[192,2,4,2,512]{4,3,0,2,1:T(2,128)(2,1)S(1)} %copy.4) | data formatting | bytes 6291456 | tf_op jit(solution)/shard_map/reshape | solution.py:142
  15.0 78.0 %all_to_all.25 = bf16[192,8,1024]{2,0,1:T(8,128)(2,1)S(1)} all-to-all(bf16[192,8,1024]{2,0,1:T(8,128)(2,1)} %reshape.21), channel_id=1, replica_groups=mesh['section'=4,'dp'=8] {'dp'}, dimensions={1} | all-to-all | bytes 6291456 | tf_op jit(solution)/shard_map/all_to_all | solution.py:143
  93.0 0.0 copy-start.2
  93.0 0.0 copy-start.3
  93.0 1.3 slice.8
  94.3 1.4 collective-permute-start.1
  95.7 0.0 copy-done.2
  95.8 6.6 %multiply_reduce_fusion = f32[2]{0:T(128)S(1)} fusion(bf16[192,2,4096]{2,1,0:T(2,128)(2,1)S(1)} %copy-done.2), kind=kLoop, calls=%fused_computation | loop fusion | flops 4718590 | bytes 3145736 | tf_op jit(solution)/shard_map/reduce_sum | solution.py:131
  102.3 19.4 %psum.7 = f32[2]{0:T(128)S(1)} all-reduce(f32[2]{0:T(128)S(1)} %multiply_reduce_fusion), channel_id=1, replica_groups=mesh['section'=4,'dp'=8] {'dp'}, use_global_device_ids=true, to_apply=%region_1.0 | all-reduce | flops 2 | bytes 16 | tf_op jit(solution)/shard_map/psum | solution.py:132
  121.8 0.0 copy-done.3
  121.8 1.5 collective-permute-start
  123.3 1.5 collective-permute-done
  124.8 0.8 pad_maximum_fusion.levels
  125.6 0.0 collective-permute-done.1.right
  125.6 34.4 %shard_map.41 = (f32[8,128,128]{2,1,0:T(8,128)S(1)}, f32[8,128,128]{2,1,0:T(8,128)S(1)}) custom-call(f32[4]{0:T(128)S(1)} %pad_maximum_fusion.levels, bf16[1536,1024]{1,0:T(8,128)(2,1)S(1)} %bitcast.13, bf16[1536,512]{1,0:T(8,128)(2,1)} %collective-permute-done.1.right), custom_call_target="tpu_custom_call" | custom-call | tf_op jit(solution)/shard_map/pallas_call | solution.py:169
  160.0 0.0 copy-start
  160.0 0.8 copy-done
  160.8 0.0 copy-start.1
  160.8 0.8 copy-done.1
  161.6 31.0 %shard_map.42 = f32[1024,128]{1,0:T(8,128)} custom-call(f32[1024,128]{1,0:T(8,128)} %bitcast.14), custom_call_target="tpu_custom_call" | custom-call | flops 201326592 | bytes 40000000 | tf_op jit(solution)/shard_map/pallas_call | solution.py:181
  192.6 17.5 %all_to_all.26 = f32[8,128,128]{2,1,0:T(8,128)S(1)} all-to-all(f32[8,128,128]{2,1,0:T(8,128)} %bitcast.16), channel_id=1, replica_groups={{0,4},{1,5},{2,6},{3,7},{8,12},{9,13},{10,14},{11,15},{16,20},{17,21},{..., dimensions={0} | all-to-all | bytes 1048576 | tf_op jit(solution)/shard_map/all_to_all | solution.py:195
  210.1 15.5 %all_to_all.27 = f32[8,128,128]{2,1,0:T(8,128)S(1)} all-to-all(f32[8,128,128]{2,1,0:T(8,128)} %copy-done), channel_id=1, replica_groups={{0,4},{1,5},{2,6},{3,7},{8,12},{9,13},{10,14},{11,15},{16,20},{17,21},{..., dimensions={0} | all-to-all | bytes 1048576 | tf_op jit(solution)/shard_map/all_to_all | solution.py:195
  225.6 0.8 copy.7
  226.4 0.8 copy.8
  (1 shorter events, 0.0 us)
Async XLA Ops:
  93.0 2.8 %copy-start.2 = (bf16[192,2,4096]{2,1,0:T(2,128)(2,1)S(1)}, bf16[192,2,4096]{2,1,0:T(2,128)(2,1)}, u32[]{:S(2)}) copy-start(bf16[192,2,4096]{2,1,0:T(2,128)(2,1)} %param.2) | copy-start | bytes 9437188
  93.0 28.8 %copy-start.3 = (f32[2]{0:T(128)S(1)}, f32[2]{0:T(128)}, u32[]{:S(2)}) copy-start(f32[2]{0:T(128)} %param.3) | copy-start | bytes 28
  94.3 31.3 %collective-permute-start.1 = (bf16[1536,512]{1,0:T(8,128)(2,1)}, bf16[1536,512]{1,0:T(8,128)(2,1)}, u32[]{:S(2)}, u32[]{:S(2)}) collective-permute-start(bf16[1536,512]{1,0:T(8,128)(2,1)} %slice.8), channel_id=1, source_target_pairs={{8,0},{16,8},{24,16},{9,1},{17,9},{25,17},{10,2},{18,10},{26,18},{... | collective-permute-start | bytes 4718600 | tf_op jit(solution)/shard_map/ppermute | solution.py:17
  121.8 3.0 %collective-permute-start = (f32[1]{0:T(128)S(1)}, f32[1]{0:T(128)}, u32[]{:S(2)}, u32[]{:S(2)}) collective-permute-start(f32[1]{0:T(128)S(1)} %bitcast.17), channel_id=1, source_target_pairs={{8,0},{16,8},{24,16},{9,1},{17,9},{25,17},{10,2},{18,10},{26,18},{... | collective-permute-start | bytes 20 | tf_op jit(solution)/shard_map/ppermute | solution.py:17
  160.0 0.8 copy-start
  160.8 0.8 copy-start.1

commit v3 on v2

--- a/solution.py
+++ b/solution.py
@@ -15,6 +15,24 @@
     devices = range(lax.axis_size(axis))
     route = [(i - distance, i) for i in devices if i - distance in devices]
     return lax.ppermute(block, axis, route)
+
+
+def handed_to_owners(blocks, layers, groups, spread):
+    pieces = blocks.reshape(layers, spread, B, B)
+    mine = lax.axis_index("dp") // groups
+    kept = lax.dynamic_index_in_dim(pieces, mine, 0)
+    result = jnp.broadcast_to(kept, pieces.shape)
+    part = jnp.arange(layers).reshape(layers, 1, 1, 1)
+    for shift in range(1, layers):
+        route = [
+            (h * groups + g, (h + shift) % layers * groups + g)
+            for h in range(layers)
+            for g in range(groups)
+        ]
+        sent = lax.dynamic_index_in_dim(pieces, (mine + shift) % layers, 0)
+        came = lax.ppermute(sent, "dp", route)
+        result = jnp.where(part == (mine - shift) % layers, came, result)
+    return result.reshape(blocks.shape)
 
 
 def three_terms(value):
@@ -190,12 +208,8 @@
     )(schur.reshape(flat.shape)).reshape(blocks)
 
     if every_layer:
-        owners = [[h * groups + g for h in range(local_layers)] for g in range(groups)]
         inverse, coupling = (
-            lax.all_to_all(
-                x, "dp", split_axis=0, concat_axis=0, tiled=True, axis_index_groups=owners
-            )
-            for x in (inverse, coupling)
+            handed_to_owners(x, local_layers, groups, spread) for x in (inverse, coupling)
         )
     return inverse, coupling
 

time: 228 us -> 209 us (0.917)
  blocking collectives: 130 us -> 97.4 us
  waiting for transfers between devices: 1.55 us -> 12.8 us
  starting transfers between devices: 2.88 us -> 5.87 us
    all_to_all x2 -> x0, blocking collectives: 33 us -> none  [local(): lax.all_to_all(x, 'dp', split_axis=0, concat_axis=0, tiled=True, axis_ind...]
    ppermute x0 -> x2, waiting for transfers between devices: none -> 11.3 us  [handed_to_owners(): came = lax.ppermute(sent, 'dp', route)]
    ppermute x0 -> x2, starting transfers between devices: none -> 2.99 us  [handed_to_owners(): came = lax.ppermute(sent, 'dp', route)]
    unnamed x10 -> x6, local copies, waits for them, and re-layouts: 3.16 us -> 0.74 us
  transfers between devices with their start and end apart: 2 -> 4, of which waited for: 1 -> 2; matrix products, arithmetic and copies ran while one was open for 3% -> 4% of each run, Pallas kernels for 0% -> 15%
where the time goes in v3:
time: 209 us; the launch traced here: 208 us
  blocking collectives  97.4 us (47%)
  Pallas kernels  65.4 us (31%)
  local copies, waits for them, and re-layouts  17.7 us (8%)
  waiting for transfers between devices  12.8 us (6%)
  other arithmetic  8.47 us (4%)
  starting transfers between devices  5.87 us (3%)
    all_to_all x1, blocking collectives, local(): lax.all_to_all(sent, 'dp', split_axis=1, concat_axis=0, tiled=True)  78 us
    pallas_call x1, Pallas kernels, local(): pl.pallas_call(functools.partial(coupling_kernel, per_device, spread, tok...  34.4 us
    pallas_call x1, Pallas kernels, local(): pl.pallas_call(functools.partial(inverse_kernel, per_device), out_shape=f...  31 us
    psum x1, blocking collectives, local(): levels = damping * lax.psum(squares, 'dp') / (tokens_all * model_width)  19.4 us
    ppermute x2, waiting for transfers between devices, handed_to_owners(): came = lax.ppermute(sent, 'dp', route)  11.3 us
    reduce_sum x1, other arithmetic, local(): squares = jnp.sum(jnp.square(activations.astype(jnp.float32)), axis=(0, 2))  6.58 us
    reshape x1, local copies, waits for them, and re-layouts, local(): activations.reshape(token_rows, local_layers, groups, local_layers, sprea...  6.17 us
    transpose x1, local copies, waits for them, and re-layouts, local(): sent = sent.transpose(0, 3, 2, 1, 4).reshape(token_rows, group_size, -1)  4.31 us
  transfers between devices with their start and end apart: 4, of which 2 were waited for; matrix products, arithmetic and copies ran while one was open for 4% of the time, Pallas kernels for 15%

profile of v3, /device:TPU:0, one launch (start us, length us, event | category | flops | bytes accessed | tf_op | source)
XLA Modules:
  0.0 208.4 jit_solution(7760478139197132455)
XLA Ops:
  0.6 6.2 %reshape.35 = bf16[192,2,4,2,512]{4,3,2,1,0:T(2,128)(2,1)} reshape(bf16[192,2,4096]{2,1,0:T(2,128)(2,1)} %param.2) | data formatting | bytes 6291456 | tf_op jit(solution)/shard_map/reshape | solution.py:157
  6.8 4.3 %copy.4 = bf16[192,2,4,2,512]{4,3,0,2,1:T(2,128)(2,1)S(1)} copy(bf16[192,2,4,2,512]{4,1,2,3,0:T(2,128)(2,1)} %bitcast.31) | data formatting | bytes 6291456 | tf_op jit(solution)/shard_map/transpose | solution.py:160
  11.1 3.9 %reshape.36 = bf16[192,8,1024]{2,0,1:T(8,128)(2,1)} reshape(bf16[192,2,4,2,512]{4,3,0,2,1:T(2,128)(2,1)S(1)} %copy.4) | data formatting | bytes 6291456 | tf_op jit(solution)/shard_map/reshape | solution.py:160
  15.0 78.0 %all_to_all.15 = bf16[192,8,1024]{2,0,1:T(8,128)(2,1)S(1)} all-to-all(bf16[192,8,1024]{2,0,1:T(8,128)(2,1)} %reshape.36), channel_id=1, replica_groups=mesh['section'=4,'dp'=8] {'dp'}, dimensions={1} | all-to-all | bytes 6291456 | tf_op jit(solution)/shard_map/all_to_all | solution.py:161
  93.0 0.0 copy-start.1
  93.0 0.0 copy-start.2
  93.0 1.3 slice.8
  94.3 1.4 collective-permute-start.1
  95.8 0.0 copy-done.1
  95.8 6.6 %multiply_reduce_fusion = f32[2]{0:T(128)S(1)} fusion(bf16[192,2,4096]{2,1,0:T(2,128)(2,1)S(1)} %copy-done.1), kind=kLoop, calls=%fused_computation | loop fusion | flops 4718590 | bytes 3145736 | tf_op jit(solution)/shard_map/reduce_sum | solution.py:149
  102.3 19.4 %psum.7 = f32[2]{0:T(128)S(1)} all-reduce(f32[2]{0:T(128)S(1)} %multiply_reduce_fusion), channel_id=1, replica_groups=mesh['section'=4,'dp'=8] {'dp'}, use_global_device_ids=true, to_apply=%region_1.0 | all-reduce | flops 2 | bytes 16 | tf_op jit(solution)/shard_map/psum | solution.py:150
  121.8 0.0 copy-done.2
  121.8 1.5 collective-permute-start
  123.3 1.5 collective-permute-done
  124.8 0.7 pad_maximum_fusion.levels
  125.6 0.0 collective-permute-done.1.right
  125.6 34.4 %shard_map.41 = (f32[8,128,128]{2,1,0:T(8,128)S(1)}, f32[8,128,128]{2,1,0:T(8,128)S(1)}) custom-call(f32[4]{0:T(128)S(1)} %pad_maximum_fusion.levels, bf16[1536,1024]{1,0:T(8,128)(2,1)S(1)} %bitcast.28, bf16[1536,512]{1,0:T(8,128)(2,1)} %collective-permute-done.1.right), custom_call_target="tpu_custom_call" | custom-call | tf_op jit(solution)/shard_map/pallas_call | solution.py:187
  160.0 0.0 copy-start
  160.0 0.7 copy-done
  160.8 0.0 collective-permute-start.3
  160.8 31.0 %shard_map.42 = f32[1024,128]{1,0:T(8,128)} custom-call(f32[1024,128]{1,0:T(8,128)} %bitcast.30), custom_call_target="tpu_custom_call" | custom-call | flops 201326592 | bytes 40000000 | tf_op jit(solution)/shard_map/pallas_call | solution.py:199
  191.8 1.1 constant_dynamic-slice_fusion.1
  192.9 3.0 %collective-permute-start.2 = (f32[1,4,128,128]{3,2,1,0:T(8,128)S(1)}, f32[1,4,128,128]{3,2,1,0:T(8,128)S(1)}, u32[]{:S(2)}, u32[]{:S(2)}) collective-permute-start(f32[1,4,128,128]{3,2,1,0:T(8,128)S(1)} %get-tuple-element.8), channel_id=1, source_target_pairs={{0,4},{1,5},{2,6},{3,7},{4,0},{5,1},{6,2},{7,3},{8,12},{9,13},{10,... | collective-permute-start | bytes 786440 | tf_op jit(solution)/shard_map/ppermute | solution.py:33
  195.9 0.1 broadcast_in_dim.60
  195.9 0.1 broadcast_in_dim.61
  196.0 0.0 collective-permute-done.3
  196.0 11.3 %collective-permute-done.2 = f32[1,4,128,128]{3,2,1,0:T(8,128)S(1)} collective-permute-done((f32[1,4,128,128]{3,2,1,0:T(8,128)S(1)}, f32[1,4,128,128]{3,2,1,0:T(8,128)S(1)}, u32[]{:S(2)}, u32[]{:S(2)}) %collective-permute-start.2) | collective-permute-done | bytes 262176 | tf_op jit(solution)/shard_map/ppermute | solution.py:33
  207.3 1.1 bitcast_select_fusion
  (3 shorter events, 0.1 us)
Async XLA Ops:
  93.0 2.8 %copy-start.1 = (bf16[192,2,4096]{2,1,0:T(2,128)(2,1)S(1)}, bf16[192,2,4096]{2,1,0:T(2,128)(2,1)}, u32[]{:S(2)}) copy-start(bf16[192,2,4096]{2,1,0:T(2,128)(2,1)} %param.2) | copy-start | bytes 9437188
  93.0 28.8 %copy-start.2 = (f32[2]{0:T(128)S(1)}, f32[2]{0:T(128)}, u32[]{:S(2)}) copy-start(f32[2]{0:T(128)} %param.3) | copy-start | bytes 28
  94.3 31.2 %collective-permute-start.1 = (bf16[1536,512]{1,0:T(8,128)(2,1)}, bf16[1536,512]{1,0:T(8,128)(2,1)}, u32[]{:S(2)}, u32[]{:S(2)}) collective-permute-start(bf16[1536,512]{1,0:T(8,128)(2,1)} %slice.8), channel_id=1, source_target_pairs={{8,0},{16,8},{24,16},{9,1},{17,9},{25,17},{10,2},{18,10},{26,18},{... | collective-permute-start | bytes 4718600 | tf_op jit(solution)/shard_map/ppermute | solution.py:17
  121.8 3.0 %collective-permute-start = (f32[1]{0:T(128)S(1)}, f32[1]{0:T(128)}, u32[]{:S(2)}, u32[]{:S(2)}) collective-permute-start(f32[1]{0:T(128)S(1)} %bitcast.35), channel_id=1, source_target_pairs={{8,0},{16,8},{24,16},{9,1},{17,9},{25,17},{10,2},{18,10},{26,18},{... | collective-permute-start | bytes 20 | tf_op jit(solution)/shard_map/ppermute | solution.py:17
  160.0 0.8 copy-start
  160.8 35.3 %collective-permute-start.3 = (f32[1,4,128,128]{3,2,1,0:T(8,128)S(1)}, f32[1,4,128,128]{3,2,1,0:T(8,128)S(1)}, u32[]{:S(2)}, u32[]{:S(2)}) collective-permute-start(f32[1,4,128,128]{3,2,1,0:T(8,128)S(1)} %get-tuple-element.6), channel_id=1, source_target_pairs={{0,4},{1,5},{2,6},{3,7},{4,0},{5,1},{6,2},{7,3},{8,12},{9,13},{10,... | collective-permute-start | bytes 786440 | tf_op jit(solution)/shard_map/ppermute | solution.py:33
  192.9 14.4 %collective-permute-start.2 = (f32[1,4,128,128]{3,2,1,0:T(8,128)S(1)}, f32[1,4,128,128]{3,2,1,0:T(8,128)S(1)}, u32[]{:S(2)}, u32[]{:S(2)}) collective-permute-start(f32[1,4,128,128]{3,2,1,0:T(8,128)S(1)} %get-tuple-element.8), channel_id=1, source_target_pairs={{0,4},{1,5},{2,6},{3,7},{4,0},{5,1},{6,2},{7,3},{8,12},{9,13},{10,... | collective-permute-start | bytes 786440 | tf_op jit(solution)/shard_map/ppermute | solution.py:33
